TPU v7x, 512 devices: a whole 4x8x8 slice. The times are simulated.
512 devices in a mesh: row: 8 (over y), col: 32 (over z, x), rep: 2 (over core).
Axes of the slice: x: 4, y: 8, z: 8, core: 2. Of those that a mesh axis runs over, the one named last changes fastest.
Arguments:
- gain: float32 [768, 8, 128, 128], P(('row', 'col'), 'rep'), as said below
- coupled_columns: int32 [768, 8], P(('row', 'col')), may hold values from 0 to 767, as said below
- solution: float32 [98304, 512], P(('row', 'col')), may hold values from -6 to 6
- residual: float32 [98304, 512], P(('row', 'col')), may hold values from -6 to 6
- direction: float32 [98304, 512], P(('row', 'col')), may hold values from -6 to 6
Outputs:
- solution_next: float32 [98304, 512], P(('row', 'col'))
- residual_next: float32 [98304, 512], P(('row', 'col'))
- direction_next: float32 [98304, 512], P(('row', 'col'))
Inputs may be any that keep to these rules, and one draw needn't show every extreme that they name: `coupled_columns`: each block row i names first its coupled block columns in ascending order (always i - 1, i, i + 1 where inside 0 to 767, some of i - 3, i - 2, i + 2, i + 3, the coupling being symmetric), at most 7 of them, and then fills the remaining slots with i itself; every named column is within 3 of i. The gain matrix assembled from its blocks is symmetric; padding slots hold zero blocks; each diagonal entry exceeds the sum of the absolute values of the other entries of its row by exactly 1.
All inputs are finite; a program needn't handle non-finite values.
Results may differ from a plain program's by a relative error of at most 0.000061.
Values sent between devices are 32-bit elements; how exact they have to be, the bound alone decides.
No kernel may reach another device: no remote copies, remote signals or barrier semaphores. Data moves between devices by JAX's collectives and lax.ppermute only.
A program may use at most 64 MiB of HBM per device.

v0:
```python
import jax
import jax.numpy as jnp
from jax import lax
from jax.experimental import pallas as pl
from jax.experimental.pallas import tpu as pltpu
from jax.sharding import Mesh
from jax.sharding import PartitionSpec as P

BLK = 128
REACH = 3
CHUNKS = 2
ROW_COL = ("row", "col_0", "col_1")
ALL = ("row", "col_0", "col_1", "rep")
F32, BF16 = jnp.float32, jnp.bfloat16


def halo_pairs(groups, first):
    pairs = []
    for rep in range(2):
        for p in range((rep + 1 - first) % 2, groups - 1, 2):
            near, far = 2 * p + rep, 2 * (p + 1) + rep
            pairs += [(near, far), (far, near)]
    return pairs


def split(x):
    top = x.astype(BF16)
    return top, (x - top.astype(F32)).astype(BF16)


def dot3(a_top, a_rest, x):
    x_top, x_rest = split(x)
    dot = lambda a, b: jnp.dot(a, b, preferred_element_type=F32)
    return dot(a_top, x_top) + (dot(a_top, x_rest) + dot(a_rest, x_top))


def take_half(direction, own, sem):
    half = own.shape[1]
    at = pl.ds(pl.multiple_of(lax.axis_index("rep") * half, half), half)
    copy = pltpu.make_async_copy(direction.at[:, at], own, sem)
    copy.start()
    copy.wait()


def place_blocks(columns, blocks, offset, dense):
    rows, slots = blocks.shape[0], blocks.shape[1]
    segment = lax.axis_index(ROW_COL)
    low_first = (segment + lax.axis_index("rep")) % 2 == 1
    for i in range(rows):
        for k in range(slots):
            w = columns[i, offset + k] - segment * rows + REACH
            low = jnp.where(low_first, w, w + 3)
            high = jnp.where(low_first, w - 3, w - 6)
            c = jnp.where(w < 3, low, jnp.where(w > 5, high, w + 3))
            here = pl.ds(i * BLK, BLK)
            dense[c, here, :] = dense[c, here, :] + blocks[i, k]


def begin(columns, gain, residual, direction, solution, dense, norm, res, dir_, sol, mine, sems):
    rep = lax.axis_index("rep")
    half = residual.shape[1] // 2
    ends = ((gain, mine), (residual, res), (direction, dir_), (solution, sol))
    copies = [pltpu.make_async_copy(*pair, sems.at[n]) for n, pair in enumerate(ends)]
    for copy in copies:
        copy.start()
    dense[...] = jnp.zeros_like(dense)
    copies[0].wait()
    place_blocks(columns, mine, rep * mine.shape[1], dense)
    copies[1].wait()
    r = res[:, pl.ds(pl.multiple_of(rep * half, half), half)]
    norm[...] = jnp.sum(r * r, axis=0, keepdims=True)
    copies[2].wait()
    copies[3].wait()


def prepare(columns, other, own, start, top_1, rest_1, top_2, rest_2, local, dense):
    dense[...] = start[...]
    place_blocks(columns, other, (1 - lax.axis_index("rep")) * other.shape[1], dense)
    for c in range(3):
        top_1[c], rest_1[c] = split(dense[c])
        top_2[c], rest_2[c] = split(dense[3 + c])
    middle = jnp.concatenate([dense[6], dense[7], dense[8]], axis=1)
    m_top, m_rest = split(middle)
    local[...] = dot3(m_top, m_rest, own[...])


def add_halo(start, x, top, rest):
    join = lambda terms: jnp.concatenate([terms[c] for c in range(3)], axis=1)
    return start[...] + dot3(join(top), join(rest), x[...])


def first_halo(one, top, rest, local, partial):
    partial[...] = add_halo(local, one, top, rest)


def finish(two, top, rest, partial, own, res, norm, image, sums):
    product = add_halo(partial, two, top, rest)
    half = product.shape[1]
    image[...] = product
    r = res[:, pl.ds(pl.multiple_of(lax.axis_index("rep") * half, half), half)]
    rows = [
        norm[...],
        jnp.sum(own[...] * product, axis=0, keepdims=True),
        jnp.sum(r * product, axis=0, keepdims=True),
        jnp.sum(product * product, axis=0, keepdims=True),
    ]
    packed = jnp.concatenate([v[:, h : h + BLK] for v in rows for h in range(0, half, BLK)], axis=0)
    sums[...] = jnp.broadcast_to(packed[None], sums.shape)


def fold(terms, sums):
    sums[...] = jnp.broadcast_to(jnp.sum(terms[...], axis=0)[None], sums.shape)


def update(terms, image, other, solution, residual, direction, sol_next, res_next, dir_next):
    half = image.shape[1]
    chunk = sol_next.shape[0]
    rep = lax.axis_index("rep")
    here = pl.ds(pl.multiple_of(pl.program_id(0) * chunk, chunk), chunk)
    for side in range(2):
        total = terms[side]
        for n in range(1, terms.shape[0] // 2):
            total += terms[2 * n + side]
        mine = rep == side
        for h in range(half // BLK):
            lanes = slice(side * half + h * BLK, side * half + (h + 1) * BLK)
            part = slice(h * BLK, (h + 1) * BLK)
            norm_old, curvature, crossing, square = (total[2 * n + h : 2 * n + h + 1] for n in range(4))
            step = norm_old / curvature
            norm_new = norm_old - 2.0 * step * crossing + step * step * square
            ratio = norm_new / norm_old
            product = jnp.where(mine, image[here, part], other[here, part])
            d = direction[here, lanes]
            sol_next[:, lanes] = solution[here, lanes] + step * d
            r = residual[here, lanes] - step * product
            res_next[:, lanes] = r
            dir_next[:, lanes] = r + ratio * d


def in_hbm(x):
    return pltpu.with_memory_space_constraint(x, pltpu.HBM)


def vmem(n):
    return [pl.BlockSpec(memory_space=pltpu.VMEM)] * n


def from_all(x, axes):
    return lax.all_to_all(x, axes, 0, 0, tiled=True)


def iteration(gain, coupled_columns, solution, residual, direction):
    rows, _ = gain.shape[:2]
    states, snapshots = direction.shape
    half = snapshots // 2
    groups = lax.axis_size(ROW_COL)

    halves = jax.ShapeDtypeStruct((states, half), F32)
    own = pl.pallas_call(
        take_half,
        out_shape=halves,
        in_specs=[pl.BlockSpec(memory_space=pltpu.HBM)],
        out_specs=vmem(1)[0],
        scratch_shapes=[pltpu.SemaphoreType.DMA],
        compiler_params=pltpu.CompilerParams(vmem_limit_bytes=2 << 20),
        name="take_half",
    )(in_hbm(direction))
    one = lax.ppermute(own, ALL, halo_pairs(groups, True))
    two = lax.ppermute(own, ALL, halo_pairs(groups, False))
    other_gain = lax.ppermute(gain, "rep", [(0, 1), (1, 0)])
    smem = pl.BlockSpec(memory_space=pltpu.SMEM)
    whole = jax.ShapeDtypeStruct((states, snapshots), F32)
    terms = jax.ShapeDtypeStruct((REACH, states, BLK), BF16)
    band = jax.ShapeDtypeStruct((3 * rows, states, BLK), F32)
    dense, norm, res, dir_, sol = pl.pallas_call(
        begin,
        out_shape=(band, jax.ShapeDtypeStruct((1, half), F32), whole, whole, whole),
        in_specs=[smem, *[pl.BlockSpec(memory_space=pltpu.HBM)] * 4],
        out_specs=tuple(vmem(5)),
        scratch_shapes=[pltpu.VMEM(gain.shape, F32), pltpu.SemaphoreType.DMA((4,))],
        cost_estimate=pl.CostEstimate(flops=4_000_000, bytes_accessed=5_000_000, transcendentals=0),
        compiler_params=pltpu.CompilerParams(vmem_limit_bytes=12 << 20),
        name="begin",
    )(in_hbm(coupled_columns), *map(in_hbm, (gain, residual, direction, solution)))
    *terms, local = pl.pallas_call(
        prepare,
        out_shape=(*[terms] * 4, halves),
        in_specs=[smem, *vmem(3)],
        out_specs=tuple(vmem(5)),
        scratch_shapes=[pltpu.VMEM(band.shape, F32)],
        cost_estimate=pl.CostEstimate(flops=400_000_000, bytes_accessed=5_000_000, transcendentals=0),
        compiler_params=pltpu.CompilerParams(vmem_limit_bytes=10 << 20),
        name="prepare",
    )(in_hbm(coupled_columns), other_gain, own, dense)

    n1 = lax.axis_size("row") * lax.axis_size("col_1")
    n2 = 2 * lax.axis_size("col_0")
    partial = pl.pallas_call(
        first_halo,
        out_shape=halves,
        in_specs=vmem(4),
        out_specs=vmem(1)[0],
        cost_estimate=pl.CostEstimate(flops=250_000_000, bytes_accessed=1_000_000, transcendentals=0),
        compiler_params=pltpu.CompilerParams(vmem_limit_bytes=8 << 20),
        name="first_halo",
    )(one, terms[0], terms[1], local)
    image, sums = pl.pallas_call(
        finish,
        out_shape=(halves, jax.ShapeDtypeStruct((n1, 8, BLK), F32)),
        in_specs=vmem(7),
        out_specs=tuple(vmem(2)),
        cost_estimate=pl.CostEstimate(flops=500_000_000, bytes_accessed=5_000_000, transcendentals=0),
        compiler_params=pltpu.CompilerParams(vmem_limit_bytes=10 << 20),
        name="finish",
    )(two, terms[2], terms[3], partial, own, res, norm)
    sums = from_all(sums, ("row", "col_1"))
    other_image = lax.ppermute(image, "rep", [(0, 1), (1, 0)])
    sums = pl.pallas_call(
        fold,
        out_shape=jax.ShapeDtypeStruct((n2, 8, BLK), F32),
        in_specs=vmem(1),
        out_specs=vmem(1)[0],
        compiler_params=pltpu.CompilerParams(vmem_limit_bytes=2 << 20),
        name="fold",
    )(sums)
    sums = from_all(sums, ("col_0", "rep"))

    chunk = states // CHUNKS
    block = pl.BlockSpec((chunk, snapshots), lambda c: (c, 0))
    return pl.pallas_call(
        update,
        grid=(CHUNKS,),
        out_shape=(whole, whole, whole),
        in_specs=vmem(6),
        out_specs=(block, block, block),
        compiler_params=pltpu.CompilerParams(vmem_limit_bytes=10 << 20),
        name="update",
    )(sums, image, other_image, sol, res, dir_)


def solution(mesh):
    finer = Mesh(
        mesh.devices.reshape(mesh.shape["row"], 8, 4, mesh.shape["rep"]),
        ALL,
    )
    return jax.shard_map(
        iteration,
        mesh=finer,
        in_specs=(
            P(ROW_COL, "rep", None, None),
            P(ROW_COL, None),
            P(ROW_COL, None),
            P(ROW_COL, None),
            P(ROW_COL, None),
        ),
        out_specs=(P(ROW_COL, None), P(ROW_COL, None), P(ROW_COL, None)),
        check_vma=False,
    )
```

profile of v0, /device:TPU:1, one launch (start us, length us, event | category | flops | bytes accessed | tf_op | source)
XLA Modules:
  0.0 65.2 jit_solution(4070999952492041037)
XLA Ops:
  0.6 8.7 %collective-permute-start.1 = (f32[3,4,128,128]{3,2,1,0:T(8,128)}, f32[3,4,128,128]{3,2,1,0:T(8,128)S(1)}, u32[]{:S(2)}, u32[]{:S(2)}) collective-permute-start(f32[3,4,128,128]{3,2,1,0:T(8,128)} %gain.1), channel_id=1, source_target_pairs={{0,1},{1,0},{2,3},{3,2},{4,5},{5,4},{6,7},{7,6},{8,9},{9,8},{10,11... | collective-permute-start | bytes 2359304 | tf_op jit(solution)/shard_map/ppermute | solution.py:170
  9.4 1.0 %take_half.1.own = f32[384,256]{1,0:T(8,128)S(1)} custom-call(f32[384,512]{1,0:T(8,128)} %direction.3), custom_call_target="tpu_custom_call" | custom-call | tf_op jit(solution)/shard_map/take_half/pallas_call | solution.py:159
  10.4 0.7 %collective-permute-start.2 = (f32[384,256]{1,0:T(8,128)S(1)}, f32[384,256]{1,0:T(8,128)S(1)}, u32[]{:S(2)}, u32[]{:S(2)}) collective-permute-start(f32[384,256]{1,0:T(8,128)S(1)} %take_half.1.own), channel_id=1, source_target_pairs={{0,2},{2,0},{4,6},{6,4},{8,10},{10,8},{12,14},{14,12},{16,18},{18,... | collective-permute-start | bytes 1179656 | tf_op jit(solution)/shard_map/ppermute | solution.py:168
  11.1 1.9 %collective-permute-start = (f32[384,256]{1,0:T(8,128)S(1)}, f32[384,256]{1,0:T(8,128)S(1)}, u32[]{:S(2)}, u32[]{:S(2)}) collective-permute-start(f32[384,256]{1,0:T(8,128)S(1)} %take_half.1.own), channel_id=1, source_target_pairs={{2,4},{4,2},{6,8},{8,6},{10,12},{12,10},{14,16},{16,14},{18,20},{2... | collective-permute-start | bytes 1179656 | tf_op jit(solution)/shard_map/ppermute | solution.py:169
  13.0 2.6 %begin.1 = (f32[9,384,128]{2,1,0:T(8,128)S(1)}, f32[1,256]{1,0:T(1,128)S(1)}, f32[384,512]{1,0:T(8,128)S(1)}, f32[384,512]{1,0:T(8,128)S(1)}, f32[384,512]{1,0:T(8,128)S(1)}) custom-call(s32[3,8]{1,0:T(4,128)} %columns.3, f32[3,4,128,128]{3,2,1,0:T(8,128)} %gain.1, f32[384,512]{1,0:T(8,128)} %residual.1, f32[384,512]{1,0:T(8,128)} %direction.3, ...), custom_call_target="tpu_custom_call" | custom-call | flops 4000000 | bytes 5000000 | tf_op jit(solution)/shard_map/begin/pallas_call | solution.py:175
  15.6 0.0 collective-permute-done.1.other
  15.6 1.6 %prepare.1 = (bf16[3,384,128]{2,1,0:T(8,128)(2,1)S(1)}, bf16[3,384,128]{2,1,0:T(8,128)(2,1)S(1)}, bf16[3,384,128]{2,1,0:T(8,128)(2,1)S(1)}, bf16[3,384,128]{2,1,0:T(8,128)(2,1)S(1)}, f32[384,256]{1,0:T(8,128)S(1)}) custom-call(s32[3,8]{1,0:T(4,128)} %columns.3, f32[3,4,128,128]{3,2,1,0:T(8,128)S(1)} %collective-permute-done.1.other, ...), custom_call_target="tpu_custom_call" | custom-call | flops 400000000 | bytes 5000000 | tf_op jit(solution)/shard_map/prepare/pallas_call | solution.py:185
  17.2 0.0 collective-permute-done.2.one
  17.2 0.5 first_halo.1.partial
  17.7 6.0 %collective-permute-done.two = f32[384,256]{1,0:T(8,128)S(1)} collective-permute-done((f32[384,256]{1,0:T(8,128)S(1)}, f32[384,256]{1,0:T(8,128)S(1)}, u32[]{:S(2)}, u32[]{:S(2)}) %collective-permute-start) | collective-permute-done | bytes 393248 | tf_op jit(solution)/shard_map/ppermute | solution.py:169
  23.7 0.6 finish.1
  24.3 2.8 %collective-permute-start.3 = (f32[384,256]{1,0:T(8,128)S(1)}, f32[384,256]{1,0:T(8,128)S(1)}, u32[]{:S(2)}, u32[]{:S(2)}) collective-permute-start(f32[384,256]{1,0:T(8,128)S(1)} %get-tuple-element.24.image), channel_id=1, source_target_pairs={{0,1},{1,0},{2,3},{3,2},{4,5},{5,4},{6,7},{7,6},{8,9},{9,8},{10,11... | collective-permute-start | bytes 1179656 | tf_op jit(solution)/shard_map/ppermute | solution.py:217
  27.1 20.4 %all_to_all.10.terms = f32[32,8,128]{2,1,0:T(8,128)S(1)} all-to-all(f32[32,8,128]{2,1,0:T(8,128)S(1)} %get-tuple-element.23), channel_id=1, replica_groups=mesh['row'=8,'col_0'=8,'col_1'=4,'rep'=2] {'row','col_1'}, dimensions={0} | all-to-all | bytes 262144 | tf_op jit(solution)/shard_map/all_to_all | solution.py:149
  47.5 16.2 %all_to_all.11.terms = f32[16,8,128]{2,1,0:T(8,128)S(1)} all-to-all(f32[16,8,128]{2,1,0:T(8,128)S(1)} %fold.1), channel_id=1, replica_groups=mesh['row'=8,'col_0'=8,'col_1'=4,'rep'=2] {'col_0','rep'}, dimensions={0} | all-to-all | bytes 131072 | tf_op jit(solution)/shard_map/all_to_all | solution.py:149
  63.7 0.0 collective-permute-done.3.other
  63.7 1.5 %update.1 = (f32[384,512]{1,0:T(8,128)}, f32[384,512]{1,0:T(8,128)}, f32[384,512]{1,0:T(8,128)}) custom-call(f32[16,8,128]{2,1,0:T(8,128)S(1)} %all_to_all.11.terms, f32[384,256]{1,0:T(8,128)S(1)} %get-tuple-element.24.image, f32[384,256]{1,0:T(8,128)S(1)} %collective-permute-done.3.other, f32[384,512]{1,0:T(8,128)S(1)} %get-tuple-element.25.solution, ...), custom_call_target="tpu_custom_call" | custom-call | tf_op jit(solution)/shard_map/update/pallas_call | solution.py:230
  (1 shorter events, 0.0 us)
Async XLA Ops:
  0.6 15.0 %collective-permute-start.1 = (f32[3,4,128,128]{3,2,1,0:T(8,128)}, f32[3,4,128,128]{3,2,1,0:T(8,128)S(1)}, u32[]{:S(2)}, u32[]{:S(2)}) collective-permute-start(f32[3,4,128,128]{3,2,1,0:T(8,128)} %gain.1), channel_id=1, source_target_pairs={{0,1},{1,0},{2,3},{3,2},{4,5},{5,4},{6,7},{7,6},{8,9},{9,8},{10,11... | collective-permute-start | bytes 2359304 | tf_op jit(solution)/shard_map/ppermute | solution.py:170
  10.4 6.8 %collective-permute-start.2 = (f32[384,256]{1,0:T(8,128)S(1)}, f32[384,256]{1,0:T(8,128)S(1)}, u32[]{:S(2)}, u32[]{:S(2)}) collective-permute-start(f32[384,256]{1,0:T(8,128)S(1)} %take_half.1.own), channel_id=1, source_target_pairs={{0,2},{2,0},{4,6},{6,4},{8,10},{10,8},{12,14},{14,12},{16,18},{18,... | collective-permute-start | bytes 1179656 | tf_op jit(solution)/shard_map/ppermute | solution.py:168
  11.1 12.6 %collective-permute-start = (f32[384,256]{1,0:T(8,128)S(1)}, f32[384,256]{1,0:T(8,128)S(1)}, u32[]{:S(2)}, u32[]{:S(2)}) collective-permute-start(f32[384,256]{1,0:T(8,128)S(1)} %take_half.1.own), channel_id=1, source_target_pairs={{2,4},{4,2},{6,8},{8,6},{10,12},{12,10},{14,16},{16,14},{18,20},{2... | collective-permute-start | bytes 1179656 | tf_op jit(solution)/shard_map/ppermute | solution.py:169
  24.3 39.4 %collective-permute-start.3 = (f32[384,256]{1,0:T(8,128)S(1)}, f32[384,256]{1,0:T(8,128)S(1)}, u32[]{:S(2)}, u32[]{:S(2)}) collective-permute-start(f32[384,256]{1,0:T(8,128)S(1)} %get-tuple-element.24.image), channel_id=1, source_target_pairs={{0,1},{1,0},{2,3},{3,2},{4,5},{5,4},{6,7},{7,6},{8,9},{9,8},{10,11... | collective-permute-start | bytes 1179656 | tf_op jit(solution)/shard_map/ppermute | solution.py:217
where the time goes:
time: 65.6 us; the launch traced here: 65.2 us
  blocking collectives  36.6 us (56%)
  starting transfers between devices  14.1 us (21%)
  Pallas kernels  7.78 us (12%)
  waiting for transfers between devices  6.01 us (9%)
  between operations  0.72 us (1%)
    all_to_all x2, blocking collectives, from_all(): return lax.all_to_all(x, axes, 0, 0, tiled=True)  36.6 us
    ppermute x1, starting transfers between devices, iteration(): other_gain = lax.ppermute(gain, 'rep', [(0, 1), (1, 0)])  8.75 us
    ppermute x1, waiting for transfers between devices, iteration(): two = lax.ppermute(own, ALL, halo_pairs(groups, False))  6 us
    ppermute x1, starting transfers between devices, iteration(): other_image = lax.ppermute(image, 'rep', [(0, 1), (1, 0)])  2.78 us
    pallas_call x1, Pallas kernels, iteration(): pl.pallas_call(begin, out_shape=(band, jax.ShapeDtypeStruct((1, half), F3...  2.57 us
    ppermute x1, starting transfers between devices, iteration(): two = lax.ppermute(own, ALL, halo_pairs(groups, False))  1.92 us
    pallas_call x1, Pallas kernels, iteration(): pl.pallas_call(prepare, out_shape=(*[terms] * 4, halves), in_specs=[smem,...  1.58 us
    pallas_call x1, Pallas kernels, iteration(): pl.pallas_call(update, grid=(CHUNKS,), out_shape=(whole, whole, whole), i...  1.54 us
  transfers between devices with their start and end apart: 4, of which 1 were waited for; matrix products, arithmetic and copies ran while one was open for 0% of the time, Pallas kernels for 9%

commit v1 on v0

--- a/solution.py
+++ b/solution.py
@@ -118,9 +118,10 @@
     rep = lax.axis_index("rep")
     here = pl.ds(pl.multiple_of(pl.program_id(0) * chunk, chunk), chunk)
     for side in range(2):
-        total = terms[side]
-        for n in range(1, terms.shape[0] // 2):
-            total += terms[2 * n + side]
+        count = terms.shape[0] // 2
+        total = terms[side * count]
+        for n in range(1, count):
+            total += terms[side * count + n]
         mine = rep == side
         for h in range(half // BLK):
             lanes = slice(side * half + h * BLK, side * half + (h + 1) * BLK)
@@ -213,7 +214,7 @@
         compiler_params=pltpu.CompilerParams(vmem_limit_bytes=10 << 20),
         name="finish",
     )(two, terms[2], terms[3], partial, own, res, norm)
-    sums = from_all(sums, ("row", "col_1"))
+    sums = from_all(sums, ("col_1", "row"))
     other_image = lax.ppermute(image, "rep", [(0, 1), (1, 0)])
     sums = pl.pallas_call(
         fold,
@@ -223,7 +224,7 @@
         compiler_params=pltpu.CompilerParams(vmem_limit_bytes=2 << 20),
         name="fold",
     )(sums)
-    sums = from_all(sums, ("col_0", "rep"))
+    sums = from_all(sums, ("rep", "col_0"))
 
     chunk = states // CHUNKS
     block = pl.BlockSpec((chunk, snapshots), lambda c: (c, 0))

time: 65.6 us -> 64.8 us (0.988)
  blocking collectives: 36.6 us -> 35.8 us
    all_to_all x2, blocking collectives: 36.6 us -> 35.8 us  [from_all(): return lax.all_to_all(x, axes, 0, 0, tiled=True)]
where the time goes in v1:
time: 64.8 us; the launch traced here: 64.5 us
  blocking collectives  35.8 us (55%)
  starting transfers between devices  14.1 us (22%)
  Pallas kernels  7.78 us (12%)
  waiting for transfers between devices  6.01 us (9%)
  between operations  0.72 us (1%)
    all_to_all x2, blocking collectives, from_all(): return lax.all_to_all(x, axes, 0, 0, tiled=True)  35.8 us
    ppermute x1, starting transfers between devices, iteration(): other_gain = lax.ppermute(gain, 'rep', [(0, 1), (1, 0)])  8.75 us
    ppermute x1, waiting for transfers between devices, iteration(): two = lax.ppermute(own, ALL, halo_pairs(groups, False))  6 us
    ppermute x1, starting transfers between devices, iteration(): other_image = lax.ppermute(image, 'rep', [(0, 1), (1, 0)])  2.78 us
    pallas_call x1, Pallas kernels, iteration(): pl.pallas_call(begin, out_shape=(band, jax.ShapeDtypeStruct((1, half), F3...  2.57 us
    ppermute x1, starting transfers between devices, iteration(): two = lax.ppermute(own, ALL, halo_pairs(groups, False))  1.92 us
    pallas_call x1, Pallas kernels, iteration(): pl.pallas_call(prepare, out_shape=(*[terms] * 4, halves), in_specs=[smem,...  1.58 us
    pallas_call x1, Pallas kernels, iteration(): pl.pallas_call(update, grid=(CHUNKS,), out_shape=(whole, whole, whole), i...  1.54 us
  transfers between devices with their start and end apart: 4, of which 1 were waited for; matrix products, arithmetic and copies ran while one was open for 0% of the time, Pallas kernels for 9%

profile of v1, /device:TPU:1, one launch (start us, length us, event | category | flops | bytes accessed | tf_op | source)
XLA Modules:
  0.0 64.5 jit_solution(14421733846889845492)
XLA Ops:
  0.6 8.7 %collective-permute-start.1 = (f32[3,4,128,128]{3,2,1,0:T(8,128)}, f32[3,4,128,128]{3,2,1,0:T(8,128)S(1)}, u32[]{:S(2)}, u32[]{:S(2)}) collective-permute-start(f32[3,4,128,128]{3,2,1,0:T(8,128)} %gain.1), channel_id=1, source_target_pairs={{0,1},{1,0},{2,3},{3,2},{4,5},{5,4},{6,7},{7,6},{8,9},{9,8},{10,11... | collective-permute-start | bytes 2359304 | tf_op jit(solution)/shard_map/ppermute | solution.py:171
  9.4 1.0 %take_half.1.own = f32[384,256]{1,0:T(8,128)S(1)} custom-call(f32[384,512]{1,0:T(8,128)} %direction.3), custom_call_target="tpu_custom_call" | custom-call | tf_op jit(solution)/shard_map/take_half/pallas_call | solution.py:160
  10.4 0.7 %collective-permute-start.2 = (f32[384,256]{1,0:T(8,128)S(1)}, f32[384,256]{1,0:T(8,128)S(1)}, u32[]{:S(2)}, u32[]{:S(2)}) collective-permute-start(f32[384,256]{1,0:T(8,128)S(1)} %take_half.1.own), channel_id=1, source_target_pairs={{0,2},{2,0},{4,6},{6,4},{8,10},{10,8},{12,14},{14,12},{16,18},{18,... | collective-permute-start | bytes 1179656 | tf_op jit(solution)/shard_map/ppermute | solution.py:169
  11.1 1.9 %collective-permute-start = (f32[384,256]{1,0:T(8,128)S(1)}, f32[384,256]{1,0:T(8,128)S(1)}, u32[]{:S(2)}, u32[]{:S(2)}) collective-permute-start(f32[384,256]{1,0:T(8,128)S(1)} %take_half.1.own), channel_id=1, source_target_pairs={{2,4},{4,2},{6,8},{8,6},{10,12},{12,10},{14,16},{16,14},{18,20},{2... | collective-permute-start | bytes 1179656 | tf_op jit(solution)/shard_map/ppermute | solution.py:170
  13.0 2.6 %begin.1 = (f32[9,384,128]{2,1,0:T(8,128)S(1)}, f32[1,256]{1,0:T(1,128)S(1)}, f32[384,512]{1,0:T(8,128)S(1)}, f32[384,512]{1,0:T(8,128)S(1)}, f32[384,512]{1,0:T(8,128)S(1)}) custom-call(s32[3,8]{1,0:T(4,128)} %columns.3, f32[3,4,128,128]{3,2,1,0:T(8,128)} %gain.1, f32[384,512]{1,0:T(8,128)} %residual.1, f32[384,512]{1,0:T(8,128)} %direction.3, ...), custom_call_target="tpu_custom_call" | custom-call | flops 4000000 | bytes 5000000 | tf_op jit(solution)/shard_map/begin/pallas_call | solution.py:176
  15.6 0.0 collective-permute-done.1.other
  15.6 1.6 %prepare.1 = (bf16[3,384,128]{2,1,0:T(8,128)(2,1)S(1)}, bf16[3,384,128]{2,1,0:T(8,128)(2,1)S(1)}, bf16[3,384,128]{2,1,0:T(8,128)(2,1)S(1)}, bf16[3,384,128]{2,1,0:T(8,128)(2,1)S(1)}, f32[384,256]{1,0:T(8,128)S(1)}) custom-call(s32[3,8]{1,0:T(4,128)} %columns.3, f32[3,4,128,128]{3,2,1,0:T(8,128)S(1)} %collective-permute-done.1.other, ...), custom_call_target="tpu_custom_call" | custom-call | flops 400000000 | bytes 5000000 | tf_op jit(solution)/shard_map/prepare/pallas_call | solution.py:186
  17.2 0.0 collective-permute-done.2.one
  17.2 0.5 first_halo.1.partial
  17.7 6.0 %collective-permute-done.two = f32[384,256]{1,0:T(8,128)S(1)} collective-permute-done((f32[384,256]{1,0:T(8,128)S(1)}, f32[384,256]{1,0:T(8,128)S(1)}, u32[]{:S(2)}, u32[]{:S(2)}) %collective-permute-start) | collective-permute-done | bytes 393248 | tf_op jit(solution)/shard_map/ppermute | solution.py:170
  23.7 0.6 finish.1
  24.3 2.8 %collective-permute-start.3 = (f32[384,256]{1,0:T(8,128)S(1)}, f32[384,256]{1,0:T(8,128)S(1)}, u32[]{:S(2)}, u32[]{:S(2)}) collective-permute-start(f32[384,256]{1,0:T(8,128)S(1)} %get-tuple-element.24.image), channel_id=1, source_target_pairs={{0,1},{1,0},{2,3},{3,2},{4,5},{5,4},{6,7},{7,6},{8,9},{9,8},{10,11... | collective-permute-start | bytes 1179656 | tf_op jit(solution)/shard_map/ppermute | solution.py:218
  27.1 19.6 %all_to_all.10.terms = f32[32,8,128]{2,1,0:T(8,128)S(1)} all-to-all(f32[32,8,128]{2,1,0:T(8,128)S(1)} %get-tuple-element.23), channel_id=1, replica_groups=mesh['row'=8,'col_0'=8,'col_1'=4,'rep'=2] {'col_1','row'}, dimensions={0} | all-to-all | bytes 262144 | tf_op jit(solution)/shard_map/all_to_all | solution.py:150
  46.7 16.2 %all_to_all.11.terms = f32[16,8,128]{2,1,0:T(8,128)S(1)} all-to-all(f32[16,8,128]{2,1,0:T(8,128)S(1)} %fold.1), channel_id=1, replica_groups=mesh['row'=8,'col_0'=8,'col_1'=4,'rep'=2] {'rep','col_0'}, dimensions={0} | all-to-all | bytes 131072 | tf_op jit(solution)/shard_map/all_to_all | solution.py:150
  62.9 0.0 collective-permute-done.3.other
  62.9 1.5 %update.1 = (f32[384,512]{1,0:T(8,128)}, f32[384,512]{1,0:T(8,128)}, f32[384,512]{1,0:T(8,128)}) custom-call(f32[16,8,128]{2,1,0:T(8,128)S(1)} %all_to_all.11.terms, f32[384,256]{1,0:T(8,128)S(1)} %get-tuple-element.24.image, f32[384,256]{1,0:T(8,128)S(1)} %collective-permute-done.3.other, f32[384,512]{1,0:T(8,128)S(1)} %get-tuple-element.25.solution, ...), custom_call_target="tpu_custom_call" | custom-call | tf_op jit(solution)/shard_map/update/pallas_call | solution.py:231
  (1 shorter events, 0.0 us)
Async XLA Ops:
  0.6 15.0 %collective-permute-start.1 = (f32[3,4,128,128]{3,2,1,0:T(8,128)}, f32[3,4,128,128]{3,2,1,0:T(8,128)S(1)}, u32[]{:S(2)}, u32[]{:S(2)}) collective-permute-start(f32[3,4,128,128]{3,2,1,0:T(8,128)} %gain.1), channel_id=1, source_target_pairs={{0,1},{1,0},{2,3},{3,2},{4,5},{5,4},{6,7},{7,6},{8,9},{9,8},{10,11... | collective-permute-start | bytes 2359304 | tf_op jit(solution)/shard_map/ppermute | solution.py:171
  10.4 6.8 %collective-permute-start.2 = (f32[384,256]{1,0:T(8,128)S(1)}, f32[384,256]{1,0:T(8,128)S(1)}, u32[]{:S(2)}, u32[]{:S(2)}) collective-permute-start(f32[384,256]{1,0:T(8,128)S(1)} %take_half.1.own), channel_id=1, source_target_pairs={{0,2},{2,0},{4,6},{6,4},{8,10},{10,8},{12,14},{14,12},{16,18},{18,... | collective-permute-start | bytes 1179656 | tf_op jit(solution)/shard_map/ppermute | solution.py:169
  11.1 12.6 %collective-permute-start = (f32[384,256]{1,0:T(8,128)S(1)}, f32[384,256]{1,0:T(8,128)S(1)}, u32[]{:S(2)}, u32[]{:S(2)}) collective-permute-start(f32[384,256]{1,0:T(8,128)S(1)} %take_half.1.own), channel_id=1, source_target_pairs={{2,4},{4,2},{6,8},{8,6},{10,12},{12,10},{14,16},{16,14},{18,20},{2... | collective-permute-start | bytes 1179656 | tf_op jit(solution)/shard_map/ppermute | solution.py:170
  24.3 38.6 %collective-permute-start.3 = (f32[384,256]{1,0:T(8,128)S(1)}, f32[384,256]{1,0:T(8,128)S(1)}, u32[]{:S(2)}, u32[]{:S(2)}) collective-permute-start(f32[384,256]{1,0:T(8,128)S(1)} %get-tuple-element.24.image), channel_id=1, source_target_pairs={{0,1},{1,0},{2,3},{3,2},{4,5},{5,4},{6,7},{7,6},{8,9},{9,8},{10,11... | collective-permute-start | bytes 1179656 | tf_op jit(solution)/shard_map/ppermute | solution.py:218

commit v2 on v1

--- a/solution.py
+++ b/solution.py
@@ -194,8 +194,8 @@
         name="prepare",
     )(in_hbm(coupled_columns), other_gain, own, dense)
 
-    n1 = lax.axis_size("row") * lax.axis_size("col_1")
-    n2 = 2 * lax.axis_size("col_0")
+    n1 = lax.axis_size("col_0") * lax.axis_size("col_1")
+    n2 = 2 * lax.axis_size("row")
     partial = pl.pallas_call(
         first_halo,
         out_shape=halves,
@@ -214,7 +214,7 @@
         compiler_params=pltpu.CompilerParams(vmem_limit_bytes=10 << 20),
         name="finish",
     )(two, terms[2], terms[3], partial, own, res, norm)
-    sums = from_all(sums, ("col_1", "row"))
+    sums = from_all(sums, ("col_1", "col_0"))
     other_image = lax.ppermute(image, "rep", [(0, 1), (1, 0)])
     sums = pl.pallas_call(
         fold,
@@ -224,7 +224,7 @@
         compiler_params=pltpu.CompilerParams(vmem_limit_bytes=2 << 20),
         name="fold",
     )(sums)
-    sums = from_all(sums, ("rep", "col_0"))
+    sums = from_all(sums, ("rep", "row"))
 
     chunk = states // CHUNKS
     block = pl.BlockSpec((chunk, snapshots), lambda c: (c, 0))

time: 64.8 us -> 64.8 us (level)
  no operation moved by 1% of the time
where the time goes in v2:
time: 64.8 us; the launch traced here: 64.5 us
  blocking collectives  35.8 us (55%)
  starting transfers between devices  14.1 us (22%)
  Pallas kernels  7.78 us (12%)
  waiting for transfers between devices  6.01 us (9%)
  between operations  0.72 us (1%)
    all_to_all x2, blocking collectives, from_all(): return lax.all_to_all(x, axes, 0, 0, tiled=True)  35.8 us
    ppermute x1, starting transfers between devices, iteration(): other_gain = lax.ppermute(gain, 'rep', [(0, 1), (1, 0)])  8.75 us
    ppermute x1, waiting for transfers between devices, iteration(): two = lax.ppermute(own, ALL, halo_pairs(groups, False))  6 us
    ppermute x1, starting transfers between devices, iteration(): other_image = lax.ppermute(image, 'rep', [(0, 1), (1, 0)])  2.78 us
    pallas_call x1, Pallas kernels, iteration(): pl.pallas_call(begin, out_shape=(band, jax.ShapeDtypeStruct((1, half), F3...  2.57 us
    ppermute x1, starting transfers between devices, iteration(): two = lax.ppermute(own, ALL, halo_pairs(groups, False))  1.92 us
    pallas_call x1, Pallas kernels, iteration(): pl.pallas_call(prepare, out_shape=(*[terms] * 4, halves), in_specs=[smem,...  1.58 us
    pallas_call x1, Pallas kernels, iteration(): pl.pallas_call(update, grid=(CHUNKS,), out_shape=(whole, whole, whole), i...  1.54 us
  transfers between devices with their start and end apart: 4, of which 1 were waited for; matrix products, arithmetic and copies ran while one was open for 0% of the time, Pallas kernels for 9%

profile of v2, /device:TPU:1, one launch (start us, length us, event | category | flops | bytes accessed | tf_op | source)
XLA Modules:
  0.0 64.5 jit_solution(8155212252711927312)
XLA Ops:
  0.6 8.7 %collective-permute-start.1 = (f32[3,4,128,128]{3,2,1,0:T(8,128)}, f32[3,4,128,128]{3,2,1,0:T(8,128)S(1)}, u32[]{:S(2)}, u32[]{:S(2)}) collective-permute-start(f32[3,4,128,128]{3,2,1,0:T(8,128)} %gain.1), channel_id=1, source_target_pairs={{0,1},{1,0},{2,3},{3,2},{4,5},{5,4},{6,7},{7,6},{8,9},{9,8},{10,11... | collective-permute-start | bytes 2359304 | tf_op jit(solution)/shard_map/ppermute | solution.py:171
  9.4 1.0 %take_half.1.own = f32[384,256]{1,0:T(8,128)S(1)} custom-call(f32[384,512]{1,0:T(8,128)} %direction.3), custom_call_target="tpu_custom_call" | custom-call | tf_op jit(solution)/shard_map/take_half/pallas_call | solution.py:160
  10.4 0.7 %collective-permute-start.2 = (f32[384,256]{1,0:T(8,128)S(1)}, f32[384,256]{1,0:T(8,128)S(1)}, u32[]{:S(2)}, u32[]{:S(2)}) collective-permute-start(f32[384,256]{1,0:T(8,128)S(1)} %take_half.1.own), channel_id=1, source_target_pairs={{0,2},{2,0},{4,6},{6,4},{8,10},{10,8},{12,14},{14,12},{16,18},{18,... | collective-permute-start | bytes 1179656 | tf_op jit(solution)/shard_map/ppermute | solution.py:169
  11.1 1.9 %collective-permute-start = (f32[384,256]{1,0:T(8,128)S(1)}, f32[384,256]{1,0:T(8,128)S(1)}, u32[]{:S(2)}, u32[]{:S(2)}) collective-permute-start(f32[384,256]{1,0:T(8,128)S(1)} %take_half.1.own), channel_id=1, source_target_pairs={{2,4},{4,2},{6,8},{8,6},{10,12},{12,10},{14,16},{16,14},{18,20},{2... | collective-permute-start | bytes 1179656 | tf_op jit(solution)/shard_map/ppermute | solution.py:170
  13.0 2.6 %begin.1 = (f32[9,384,128]{2,1,0:T(8,128)S(1)}, f32[1,256]{1,0:T(1,128)S(1)}, f32[384,512]{1,0:T(8,128)S(1)}, f32[384,512]{1,0:T(8,128)S(1)}, f32[384,512]{1,0:T(8,128)S(1)}) custom-call(s32[3,8]{1,0:T(4,128)} %columns.3, f32[3,4,128,128]{3,2,1,0:T(8,128)} %gain.1, f32[384,512]{1,0:T(8,128)} %residual.1, f32[384,512]{1,0:T(8,128)} %direction.3, ...), custom_call_target="tpu_custom_call" | custom-call | flops 4000000 | bytes 5000000 | tf_op jit(solution)/shard_map/begin/pallas_call | solution.py:176
  15.6 0.0 collective-permute-done.1.other
  15.6 1.6 %prepare.1 = (bf16[3,384,128]{2,1,0:T(8,128)(2,1)S(1)}, bf16[3,384,128]{2,1,0:T(8,128)(2,1)S(1)}, bf16[3,384,128]{2,1,0:T(8,128)(2,1)S(1)}, bf16[3,384,128]{2,1,0:T(8,128)(2,1)S(1)}, f32[384,256]{1,0:T(8,128)S(1)}) custom-call(s32[3,8]{1,0:T(4,128)} %columns.3, f32[3,4,128,128]{3,2,1,0:T(8,128)S(1)} %collective-permute-done.1.other, ...), custom_call_target="tpu_custom_call" | custom-call | flops 400000000 | bytes 5000000 | tf_op jit(solution)/shard_map/prepare/pallas_call | solution.py:186
  17.2 0.0 collective-permute-done.2.one
  17.2 0.5 first_halo.1.partial
  17.7 6.0 %collective-permute-done.two = f32[384,256]{1,0:T(8,128)S(1)} collective-permute-done((f32[384,256]{1,0:T(8,128)S(1)}, f32[384,256]{1,0:T(8,128)S(1)}, u32[]{:S(2)}, u32[]{:S(2)}) %collective-permute-start) | collective-permute-done | bytes 393248 | tf_op jit(solution)/shard_map/ppermute | solution.py:170
  23.7 0.6 finish.1
  24.3 2.8 %collective-permute-start.3 = (f32[384,256]{1,0:T(8,128)S(1)}, f32[384,256]{1,0:T(8,128)S(1)}, u32[]{:S(2)}, u32[]{:S(2)}) collective-permute-start(f32[384,256]{1,0:T(8,128)S(1)} %get-tuple-element.24.image), channel_id=1, source_target_pairs={{0,1},{1,0},{2,3},{3,2},{4,5},{5,4},{6,7},{7,6},{8,9},{9,8},{10,11... | collective-permute-start | bytes 1179656 | tf_op jit(solution)/shard_map/ppermute | solution.py:218
  27.1 19.7 %all_to_all.10.terms = f32[32,8,128]{2,1,0:T(8,128)S(1)} all-to-all(f32[32,8,128]{2,1,0:T(8,128)S(1)} %get-tuple-element.23), channel_id=1, replica_groups=mesh['row'=8,'col_0'=8,'col_1'=4,'rep'=2] {'col_1','col_0'}, dimensions={0} | all-to-all | bytes 262144 | tf_op jit(solution)/shard_map/all_to_all | solution.py:150
  46.8 16.1 %all_to_all.11.terms = f32[16,8,128]{2,1,0:T(8,128)S(1)} all-to-all(f32[16,8,128]{2,1,0:T(8,128)S(1)} %fold.1), channel_id=1, replica_groups=mesh['row'=8,'col_0'=8,'col_1'=4,'rep'=2] {'rep','row'}, dimensions={0} | all-to-all | bytes 131072 | tf_op jit(solution)/shard_map/all_to_all | solution.py:150
  62.9 0.0 collective-permute-done.3.other
  62.9 1.5 %update.1 = (f32[384,512]{1,0:T(8,128)}, f32[384,512]{1,0:T(8,128)}, f32[384,512]{1,0:T(8,128)}) custom-call(f32[16,8,128]{2,1,0:T(8,128)S(1)} %all_to_all.11.terms, f32[384,256]{1,0:T(8,128)S(1)} %get-tuple-element.24.image, f32[384,256]{1,0:T(8,128)S(1)} %collective-permute-done.3.other, f32[384,512]{1,0:T(8,128)S(1)} %get-tuple-element.25.solution, ...), custom_call_target="tpu_custom_call" | custom-call | tf_op jit(solution)/shard_map/update/pallas_call | solution.py:231
  (1 shorter events, 0.0 us)
Async XLA Ops:
  0.6 15.0 %collective-permute-start.1 = (f32[3,4,128,128]{3,2,1,0:T(8,128)}, f32[3,4,128,128]{3,2,1,0:T(8,128)S(1)}, u32[]{:S(2)}, u32[]{:S(2)}) collective-permute-start(f32[3,4,128,128]{3,2,1,0:T(8,128)} %gain.1), channel_id=1, source_target_pairs={{0,1},{1,0},{2,3},{3,2},{4,5},{5,4},{6,7},{7,6},{8,9},{9,8},{10,11... | collective-permute-start | bytes 2359304 | tf_op jit(solution)/shard_map/ppermute | solution.py:171
  10.4 6.8 %collective-permute-start.2 = (f32[384,256]{1,0:T(8,128)S(1)}, f32[384,256]{1,0:T(8,128)S(1)}, u32[]{:S(2)}, u32[]{:S(2)}) collective-permute-start(f32[384,256]{1,0:T(8,128)S(1)} %take_half.1.own), channel_id=1, source_target_pairs={{0,2},{2,0},{4,6},{6,4},{8,10},{10,8},{12,14},{14,12},{16,18},{18,... | collective-permute-start | bytes 1179656 | tf_op jit(solution)/shard_map/ppermute | solution.py:169
  11.1 12.6 %collective-permute-start = (f32[384,256]{1,0:T(8,128)S(1)}, f32[384,256]{1,0:T(8,128)S(1)}, u32[]{:S(2)}, u32[]{:S(2)}) collective-permute-start(f32[384,256]{1,0:T(8,128)S(1)} %take_half.1.own), channel_id=1, source_target_pairs={{2,4},{4,2},{6,8},{8,6},{10,12},{12,10},{14,16},{16,14},{18,20},{2... | collective-permute-start | bytes 1179656 | tf_op jit(solution)/shard_map/ppermute | solution.py:170
  24.3 38.6 %collective-permute-start.3 = (f32[384,256]{1,0:T(8,128)S(1)}, f32[384,256]{1,0:T(8,128)S(1)}, u32[]{:S(2)}, u32[]{:S(2)}) collective-permute-start(f32[384,256]{1,0:T(8,128)S(1)} %get-tuple-element.24.image), channel_id=1, source_target_pairs={{0,1},{1,0},{2,3},{3,2},{4,5},{5,4},{6,7},{7,6},{8,9},{9,8},{10,11... | collective-permute-start | bytes 1179656 | tf_op jit(solution)/shard_map/ppermute | solution.py:218

commit v3 on v2

--- a/solution.py
+++ b/solution.py
@@ -15,11 +15,12 @@
 
 
 def halo_pairs(groups, first):
+    step = 1 if first else -1
     pairs = []
-    for rep in range(2):
-        for p in range((rep + 1 - first) % 2, groups - 1, 2):
-            near, far = 2 * p + rep, 2 * (p + 1) + rep
-            pairs += [(near, far), (far, near)]
+    for p in range(groups):
+        for rep, to in ((0, p + step), (1, p - step)):
+            if 0 <= to < groups:
+                pairs.append((2 * p + rep, 2 * to + rep))
     return pairs
 
 
@@ -45,7 +46,7 @@
 def place_blocks(columns, blocks, offset, dense):
     rows, slots = blocks.shape[0], blocks.shape[1]
     segment = lax.axis_index(ROW_COL)
-    low_first = (segment + lax.axis_index("rep")) % 2 == 1
+    low_first = lax.axis_index("rep") == 0
     for i in range(rows):
         for k in range(slots):
             w = columns[i, offset + k] - segment * rows + REACH

time: 64.8 us -> 64.8 us (level)
  waiting for transfers between devices: 6.01 us -> 1.75 us
  starting transfers between devices: 14.1 us -> 17.7 us
  blocking collectives: 35.8 us -> 36.5 us
    ppermute x1, waiting for transfers between devices: 6 us -> 0.01 us  [iteration(): two = lax.ppermute(own, ALL, halo_pairs(groups, False))]
    ppermute x1, starting transfers between devices: 1.92 us -> 4.01 us  [iteration(): two = lax.ppermute(own, ALL, halo_pairs(groups, False))]
    ppermute x1, waiting for transfers between devices: 0.01 us -> 1.74 us  [iteration(): one = lax.ppermute(own, ALL, halo_pairs(groups, True))]
    ppermute x1, starting transfers between devices: 2.78 us -> 3.62 us  [iteration(): other_image = lax.ppermute(image, 'rep', [(0, 1), (1, 0)])]
    all_to_all x2, blocking collectives: 35.8 us -> 36.5 us  [from_all(): return lax.all_to_all(x, axes, 0, 0, tiled=True)]
where the time goes in v3:
time: 64.8 us; the launch traced here: 64.5 us
  blocking collectives  36.5 us (56%)
  starting transfers between devices  17.7 us (27%)
  Pallas kernels  7.77 us (12%)
  waiting for transfers between devices  1.75 us (3%)
  between operations  0.72 us (1%)
    all_to_all x2, blocking collectives, from_all(): return lax.all_to_all(x, axes, 0, 0, tiled=True)  36.5 us
    ppermute x1, starting transfers between devices, iteration(): other_gain = lax.ppermute(gain, 'rep', [(0, 1), (1, 0)])  8.75 us
    ppermute x1, starting transfers between devices, iteration(): two = lax.ppermute(own, ALL, halo_pairs(groups, False))  4.01 us
    ppermute x1, starting transfers between devices, iteration(): other_image = lax.ppermute(image, 'rep', [(0, 1), (1, 0)])  3.62 us
    pallas_call x1, Pallas kernels, iteration(): pl.pallas_call(begin, out_shape=(band, jax.ShapeDtypeStruct((1, half), F3...  2.57 us
    ppermute x1, waiting for transfers between devices, iteration(): one = lax.ppermute(own, ALL, halo_pairs(groups, True))  1.74 us
    pallas_call x1, Pallas kernels, iteration(): pl.pallas_call(prepare, out_shape=(*[terms] * 4, halves), in_specs=[smem,...  1.57 us
    pallas_call x1, Pallas kernels, iteration(): pl.pallas_call(update, grid=(CHUNKS,), out_shape=(whole, whole, whole), i...  1.54 us
  transfers between devices with their start and end apart: 4, of which 1 were waited for; matrix products, arithmetic and copies ran while one was open for 0% of the time, Pallas kernels for 9%

profile of v3, /device:TPU:1, one launch (start us, length us, event | category | flops | bytes accessed | tf_op | source)
XLA Modules:
  0.0 64.5 jit_solution(15302098864452588865)
XLA Ops:
  0.6 8.7 %collective-permute-start.1 = (f32[3,4,128,128]{3,2,1,0:T(8,128)}, f32[3,4,128,128]{3,2,1,0:T(8,128)S(1)}, u32[]{:S(2)}, u32[]{:S(2)}) collective-permute-start(f32[3,4,128,128]{3,2,1,0:T(8,128)} %gain.1), channel_id=1, source_target_pairs={{0,1},{1,0},{2,3},{3,2},{4,5},{5,4},{6,7},{7,6},{8,9},{9,8},{10,11... | collective-permute-start | bytes 2359304 | tf_op jit(solution)/shard_map/ppermute | solution.py:172
  9.4 1.0 %take_half.1.own = f32[384,256]{1,0:T(8,128)S(1)} custom-call(f32[384,512]{1,0:T(8,128)} %direction.3), custom_call_target="tpu_custom_call" | custom-call | tf_op jit(solution)/shard_map/take_half/pallas_call | solution.py:161
  10.4 1.3 %collective-permute-start.2 = (f32[384,256]{1,0:T(8,128)S(1)}, f32[384,256]{1,0:T(8,128)S(1)}, u32[]{:S(2)}, u32[]{:S(2)}) collective-permute-start(f32[384,256]{1,0:T(8,128)S(1)} %take_half.1.own), channel_id=1, source_target_pairs={{0,2},{2,4},{3,1},{4,6},{5,3},{6,8},{7,5},{8,10},{9,7},{10,12},{11... | collective-permute-start | bytes 1179656 | tf_op jit(solution)/shard_map/ppermute | solution.py:170
  11.7 4.0 %collective-permute-start = (f32[384,256]{1,0:T(8,128)S(1)}, f32[384,256]{1,0:T(8,128)S(1)}, u32[]{:S(2)}, u32[]{:S(2)}) collective-permute-start(f32[384,256]{1,0:T(8,128)S(1)} %take_half.1.own), channel_id=1, source_target_pairs={{1,3},{2,0},{3,5},{4,2},{5,7},{6,4},{7,9},{8,6},{9,11},{10,8},{11,... | collective-permute-start | bytes 1179656 | tf_op jit(solution)/shard_map/ppermute | solution.py:171
  15.7 2.6 %begin.1 = (f32[9,384,128]{2,1,0:T(8,128)S(1)}, f32[1,256]{1,0:T(1,128)S(1)}, f32[384,512]{1,0:T(8,128)S(1)}, f32[384,512]{1,0:T(8,128)S(1)}, f32[384,512]{1,0:T(8,128)S(1)}) custom-call(s32[3,8]{1,0:T(4,128)} %columns.3, f32[3,4,128,128]{3,2,1,0:T(8,128)} %gain.1, f32[384,512]{1,0:T(8,128)} %residual.1, f32[384,512]{1,0:T(8,128)} %direction.3, ...), custom_call_target="tpu_custom_call" | custom-call | flops 4000000 | bytes 5000000 | tf_op jit(solution)/shard_map/begin/pallas_call | solution.py:177
  18.3 0.0 collective-permute-done.1.other
  18.3 1.6 %prepare.1 = (bf16[3,384,128]{2,1,0:T(8,128)(2,1)S(1)}, bf16[3,384,128]{2,1,0:T(8,128)(2,1)S(1)}, bf16[3,384,128]{2,1,0:T(8,128)(2,1)S(1)}, bf16[3,384,128]{2,1,0:T(8,128)(2,1)S(1)}, f32[384,256]{1,0:T(8,128)S(1)}) custom-call(s32[3,8]{1,0:T(4,128)} %columns.3, f32[3,4,128,128]{3,2,1,0:T(8,128)S(1)} %collective-permute-done.1.other, ...), custom_call_target="tpu_custom_call" | custom-call | flops 400000000 | bytes 5000000 | tf_op jit(solution)/shard_map/prepare/pallas_call | solution.py:187
  19.9 1.7 %collective-permute-done.2.one = f32[384,256]{1,0:T(8,128)S(1)} collective-permute-done((f32[384,256]{1,0:T(8,128)S(1)}, f32[384,256]{1,0:T(8,128)S(1)}, u32[]{:S(2)}, u32[]{:S(2)}) %collective-permute-start.2) | collective-permute-done | bytes 393248 | tf_op jit(solution)/shard_map/ppermute | solution.py:170
  21.6 0.5 first_halo.1.partial
  22.1 0.0 collective-permute-done.two
  22.1 0.6 finish.1
  22.7 3.6 %collective-permute-start.3 = (f32[384,256]{1,0:T(8,128)S(1)}, f32[384,256]{1,0:T(8,128)S(1)}, u32[]{:S(2)}, u32[]{:S(2)}) collective-permute-start(f32[384,256]{1,0:T(8,128)S(1)} %get-tuple-element.24.image), channel_id=1, source_target_pairs={{0,1},{1,0},{2,3},{3,2},{4,5},{5,4},{6,7},{7,6},{8,9},{9,8},{10,11... | collective-permute-start | bytes 1179656 | tf_op jit(solution)/shard_map/ppermute | solution.py:219
  26.3 20.4 %all_to_all.10.terms = f32[32,8,128]{2,1,0:T(8,128)S(1)} all-to-all(f32[32,8,128]{2,1,0:T(8,128)S(1)} %get-tuple-element.23), channel_id=1, replica_groups=mesh['row'=8,'col_0'=8,'col_1'=4,'rep'=2] {'col_1','col_0'}, dimensions={0} | all-to-all | bytes 262144 | tf_op jit(solution)/shard_map/all_to_all | solution.py:151
  46.8 16.1 %all_to_all.11.terms = f32[16,8,128]{2,1,0:T(8,128)S(1)} all-to-all(f32[16,8,128]{2,1,0:T(8,128)S(1)} %fold.1), channel_id=1, replica_groups=mesh['row'=8,'col_0'=8,'col_1'=4,'rep'=2] {'rep','row'}, dimensions={0} | all-to-all | bytes 131072 | tf_op jit(solution)/shard_map/all_to_all | solution.py:151
  62.9 0.0 collective-permute-done.3.other
  62.9 1.5 %update.1 = (f32[384,512]{1,0:T(8,128)}, f32[384,512]{1,0:T(8,128)}, f32[384,512]{1,0:T(8,128)}) custom-call(f32[16,8,128]{2,1,0:T(8,128)S(1)} %all_to_all.11.terms, f32[384,256]{1,0:T(8,128)S(1)} %get-tuple-element.24.image, f32[384,256]{1,0:T(8,128)S(1)} %collective-permute-done.3.other, f32[384,512]{1,0:T(8,128)S(1)} %get-tuple-element.25.solution, ...), custom_call_target="tpu_custom_call" | custom-call | tf_op jit(solution)/shard_map/update/pallas_call | solution.py:232
  (1 shorter events, 0.0 us)
Async XLA Ops:
  0.6 17.7 %collective-permute-start.1 = (f32[3,4,128,128]{3,2,1,0:T(8,128)}, f32[3,4,128,128]{3,2,1,0:T(8,128)S(1)}, u32[]{:S(2)}, u32[]{:S(2)}) collective-permute-start(f32[3,4,128,128]{3,2,1,0:T(8,128)} %gain.1), channel_id=1, source_target_pairs={{0,1},{1,0},{2,3},{3,2},{4,5},{5,4},{6,7},{7,6},{8,9},{9,8},{10,11... | collective-permute-start | bytes 2359304 | tf_op jit(solution)/shard_map/ppermute | solution.py:172
  10.4 11.2 %collective-permute-start.2 = (f32[384,256]{1,0:T(8,128)S(1)}, f32[384,256]{1,0:T(8,128)S(1)}, u32[]{:S(2)}, u32[]{:S(2)}) collective-permute-start(f32[384,256]{1,0:T(8,128)S(1)} %take_half.1.own), channel_id=1, source_target_pairs={{0,2},{2,4},{3,1},{4,6},{5,3},{6,8},{7,5},{8,10},{9,7},{10,12},{11... | collective-permute-start | bytes 1179656 | tf_op jit(solution)/shard_map/ppermute | solution.py:170
  11.7 10.4 %collective-permute-start = (f32[384,256]{1,0:T(8,128)S(1)}, f32[384,256]{1,0:T(8,128)S(1)}, u32[]{:S(2)}, u32[]{:S(2)}) collective-permute-start(f32[384,256]{1,0:T(8,128)S(1)} %take_half.1.own), channel_id=1, source_target_pairs={{1,3},{2,0},{3,5},{4,2},{5,7},{6,4},{7,9},{8,6},{9,11},{10,8},{11,... | collective-permute-start | bytes 1179656 | tf_op jit(solution)/shard_map/ppermute | solution.py:171
  22.7 40.2 %collective-permute-start.3 = (f32[384,256]{1,0:T(8,128)S(1)}, f32[384,256]{1,0:T(8,128)S(1)}, u32[]{:S(2)}, u32[]{:S(2)}) collective-permute-start(f32[384,256]{1,0:T(8,128)S(1)} %get-tuple-element.24.image), channel_id=1, source_target_pairs={{0,1},{1,0},{2,3},{3,2},{4,5},{5,4},{6,7},{7,6},{8,9},{9,8},{10,11... | collective-permute-start | bytes 1179656 | tf_op jit(solution)/shard_map/ppermute | solution.py:219
